TPU v7x, 32 devices: a whole 2x2x4 slice. The times are simulated.
32 devices in a mesh: blk: 4 (over y, x), grp: 8 (over z, core).
Axes of the slice: x: 2, y: 2, z: 4, core: 2. Of those that a mesh axis runs over, the one named last changes fastest.
Arguments:
- points: float32 [3, 4096], P(None, ('blk', 'grp')), may hold values from 0 to 1
- labels: int32 [4096], P(('blk', 'grp')), may hold values 0 or 1
- shape_scale: float32 [4096], P(('blk', 'grp')), may hold values from 0.1 to 0.4
- krylov_basis: float32 [8, 32, 4096], P(None, None, ('blk', 'grp')), may hold values from -6 to 6
- sketch: float32 [1024, 4096], P(None, ('blk', 'grp')), may hold values from -0.09375 to 0.09375
- sketched_basis: float32 [8, 32, 1024], replicated, may hold values from -0.1875 to 0.1875
Outputs:
- next_vector: float32 [32, 4096], P(None, ('blk', 'grp'))
- coefficients: float32 [8, 32], replicated
- sketch_next: float32 [32, 1024], replicated
- norms: float32 [32], replicated
All inputs are finite; a program needn't handle non-finite values. No bound on the sum of `labels` on one device may be relied on, other than what follows from the above.
Results may differ from a plain program's by a relative error of at most 0.0003.
Values sent between devices are 32-bit elements; how exact they have to be, the bound alone decides.
A program may use at most 64 MiB of HBM per device.

v0:
```python
import math
import jax
import jax.numpy as jnp
from jax import lax
from jax.sharding import PartitionSpec as P

SYSTEMS = 32
KRYLOV = 8


def kernel_terms(target_points, target_labels, source_block):
    source_points = source_block[0:3]
    scales = source_block[3]
    weights_block = source_block[4:]
    delta_x = source_points[0][:, None] - target_points[0][None, :]
    delta_y = source_points[1][:, None] - target_points[1][None, :]
    delta_z = source_points[2][:, None] - target_points[2][None, :]
    radius_sq = delta_x * delta_x + delta_y * delta_y + delta_z * delta_z
    squared_scale = (scales * scales)[:, None]
    shifted = radius_sq + squared_scale
    inverse = lax.rsqrt(shifted)
    boundary = shifted * inverse
    interior = (3.0 * squared_scale + 2.0 * radius_sq) * inverse * inverse * inverse
    kernel = jnp.where(target_labels[None, :] == 1, interior, boundary)
    return jnp.dot(
        weights_block, kernel, precision=lax.Precision.HIGHEST, preferred_element_type=jnp.float32
    )


def block_size(length, wanted):
    return wanted if length % wanted == 0 else length


def accumulate(running, target_points, target_labels, source_block):
    target_count = target_points.shape[1]
    source_count = source_block.shape[1]
    tblock = block_size(target_count, 2048)
    sblock = block_size(source_count, 2048)
    system_rows = running.shape[0]

    def over_targets(target_index, current):

        def over_sources(source_index, partial_value):
            portion = lax.dynamic_slice_in_dim(source_block, source_index * sblock, sblock, 1)
            return partial_value + kernel_terms(target_points, target_labels, portion)

        partial_value = lax.fori_loop(
            0, source_count // sblock, over_sources, jnp.zeros((system_rows, tblock), jnp.float32)
        )
        return current + partial_value

    return lax.fori_loop(0, target_count // tblock, over_targets, running)


def shards(points, labels, shape_scale, krylov_basis, sketch, sketched_basis):
    own_count = points.shape[1]
    everything = lax.axis_size("blk") * lax.axis_size("grp") * own_count
    sources = jnp.concatenate([points, shape_scale[None, :], krylov_basis[KRYLOV - 1]], axis=0)
    empty = jnp.zeros((SYSTEMS, own_count), jnp.float32)
    summed = accumulate(
        empty, points, labels, lax.all_gather(sources, ("blk", "grp"), axis=1, tiled=True)
    )
    image = summed / math.sqrt(everything)
    local_sketch = lax.dot_general(
        image,
        sketch,
        (((1,), (1,)), ((), ())),
        precision=lax.Precision.HIGHEST,
        preferred_element_type=jnp.float32,
    )
    sketched = lax.psum(local_sketch, ("blk", "grp"))
    coefficients = jnp.einsum(
        "jrk,rk->jr", sketched_basis, sketched, precision=lax.Precision.HIGHEST
    )
    remainder = sketched - jnp.einsum(
        "jr,jrk->rk", coefficients, sketched_basis, precision=lax.Precision.HIGHEST
    )
    norms = jnp.sqrt(jnp.mean(remainder * remainder, axis=1) + 1e-06)
    sketch_next = remainder / norms[:, None]
    reduced = image - jnp.einsum(
        "jr,jrn->rn", coefficients, krylov_basis, precision=lax.Precision.HIGHEST
    )
    next_vector = reduced / norms[:, None]
    return (next_vector, coefficients, sketch_next, norms)


def solution(mesh):
    placed = (
        P(None, ("blk", "grp")),
        P(("blk", "grp")),
        P(("blk", "grp")),
        P(None, None, ("blk", "grp")),
        P(None, ("blk", "grp")),
        P(),
    )
    return jax.shard_map(
        shards,
        mesh=mesh,
        in_specs=placed,
        out_specs=(P(None, ("blk", "grp")), P(), P(), P()),
        check_vma=False,
    )
```

profile of v0, /device:TPU:0, one launch (start us, length us, event | category | flops | bytes accessed | tf_op | source)
XLA Modules:
  0.0 195.9 jit_solution(17373773227067051160)
XLA Ops:
  7.2 0.0 copy-start
  7.2 0.0 all-reduce.2.cloned.1.call-start
  7.2 0.0 copy-start.4
  7.2 0.8 slice_bitcast_fusion.3
  8.0 0.0 copy-start.7
  8.1 0.0 copy-done.4
  8.1 0.7 copy-done.7
  8.7 45.9 %all_gather.3 = f32[36,4096]{1,0:T(8,128)S(1)} all-gather(f32[36,128]{1,0:T(8,128)S(1)} %pad_maximum_fusion), channel_id=1, replica_groups=mesh['blk'=4,'grp'=8] {'blk','grp'}, dimensions={1}, use_global_device_ids=true | all-gather | bytes 608256 | tf_op jit(solution)/shard_map/all_gather | solution.py:61
  54.7 0.0 copy-done.8
  54.7 4.4 %while.21 = (s32[]{:T(128)}, f32[32,128]{1,0:T(8,128)S(1)}, f32[36,4096]{1,0:T(8,128)S(1)}, s32[128]{0:T(128)S(1)}, f32[3,128]{1,0:T(4,128)S(1)}, /*index=5*/s32...) while((s32[]{:T(128)}, f32[32,128]{1,0:T(8,128)S(1)}, ...), condition=%wide.region_1.0_spmd.clone, body=%wide.region_0.1_spmd.clone.sunk | while | flops 104870024 | bytes 423813 | solution.py:47
  54.7 0.1 constant_dynamic-slice_fusion.2
  54.8 2.0 %convolution_add_fusion.2 = f32[32,128]{1,0:T(8,128)S(1)} fusion(f32[2048]{0:T(1024)S(1)} %bitcast.42, f32[128]{0:T(128)S(1)} %get-tuple-element.195, f32[2048]{0:T(1024)S(1)} %bitcast.45, f32[128]{0:T(128)S(1)} %get-tuple-element.197, f32[2048]{0:T(1024)S(1)} %bitcast.44, f32[128]{0:T(128)S(1)} %get-tuple-element.199, f32[2048]{0:T(1024)S(1)} %bitcast.43, ...), kind=kOutput, calls=%fused_computation.2.clone.1 | convolution fusion | flops 104865792 | bytes 337929 | tf_op jit(solution)/shard_map/while/body/eval_jaxpr/while/body/eval_jaxpr/dot_general | solution.py:25
  56.9 0.1 constant_dynamic-slice_fusion.2
  57.0 2.0 %convolution_add_fusion.2 = f32[32,128]{1,0:T(8,128)S(1)} fusion(f32[2048]{0:T(1024)S(1)} %bitcast.42, f32[128]{0:T(128)S(1)} %get-tuple-element.195, f32[2048]{0:T(1024)S(1)} %bitcast.45, f32[128]{0:T(128)S(1)} %get-tuple-element.197, f32[2048]{0:T(1024)S(1)} %bitcast.44, f32[128]{0:T(128)S(1)} %get-tuple-element.199, f32[2048]{0:T(1024)S(1)} %bitcast.43, ...), kind=kOutput, calls=%fused_computation.2.clone.1 | convolution fusion | flops 104865792 | bytes 337929 | tf_op jit(solution)/shard_map/while/body/eval_jaxpr/while/body/eval_jaxpr/dot_general | solution.py:25
  59.1 0.0 copy-done.2
  59.1 1.3 fusion.32
  60.3 0.0 all-reduce.2.cloned.1.call-update
  60.4 120.9 %all-reduce.2.cloned.1.call-done = f32[32,1024]{1,0:T(8,128)} async-done(((f32[32,1024]{1,0:T(8,128)}), f32[32,1024]{1,0:T(8,128)}) %all-reduce.2.cloned.1.call-update) | async-done | bytes 131088 | tf_op jit(solution)/shard_map/psum | solution.py:71
  181.2 0.0 copy-done
  181.3 3.6 %fusion.27 = f32[32,1,8]{2,1,0:T(1,128)S(1)} fusion(f32[8,32,1024]{2,1,0:T(8,128)S(1)} %copy-done, f32[32,1024,1]{1,0,2:T(8,128)} %bitcast.40), kind=kOutput, calls=%fused_computation.36 | convolution fusion | flops 3145728 | bytes 1180672 | tf_op jit(solution)/shard_map/jrk,rk->jr/dot_general | solution.py:72
  184.8 0.1 copy.12
  184.9 0.1 copy.13
  185.0 0.5 copy-done.5
  185.5 0.0 copy-done.3
  185.5 0.4 fusion.29
  185.9 0.0 copy-start.1
  185.9 1.5 fusion.25
  187.4 0.0 copy-done.1
  187.4 0.1 multiply_reduce_fusion
  187.6 0.7 subtract_divide_fusion
  188.3 0.0 copy-done.6
  188.3 0.7 broadcast_divide_fusion
  (14 shorter events, 0.1 us)
Async XLA Ops:
  7.2 174.1 %copy-start = (f32[8,32,1024]{2,1,0:T(8,128)S(1)}, f32[8,32,1024]{2,1,0:T(8,128)}, u32[]{:S(2)}) copy-start(f32[8,32,1024]{2,1,0:T(8,128)} %param.13) | copy-start | bytes 3145732
  7.2 174.1 %all-reduce.2.cloned.1.call-start = ((), (), s32[]{:S(2)}) async-start(), calls=%async_computation | async-start | bytes 262144 | tf_op jit(solution)/shard_map/psum | solution.py:71
  7.2 0.8 copy-start.4
  8.0 0.7 copy-start.7
  8.7 46.0 %copy-start.8 = (s32[128]{0:T(128)S(1)}, s32[128]{0:T(128)}, u32[]{:S(2)}) copy-start(s32[128]{0:T(128)} %param.9) | copy-start | bytes 1540
  54.7 4.4 %copy-start.2 = (f32[1024,128]{1,0:T(8,128)S(1)}, f32[1024,128]{1,0:T(8,128)}, u32[]{:S(2)}) copy-start(f32[1024,128]{1,0:T(8,128)} %param.12) | copy-start | bytes 1572868
  181.2 4.3 %copy-start.3 = (f32[8,32,128]{2,1,0:T(8,128)S(1)}, f32[8,32,128]{2,1,0:T(8,128)}, u32[]{:S(2)}) copy-start(f32[8,32,128]{2,1,0:T(8,128)} %param.11) | copy-start | bytes 393220
  184.9 0.6 copy-start.5
  185.9 1.5 copy-start.1
  187.6 0.7 copy-start.6
Sparse Core Ops, SparseCore 0:
  60.5 120.7 all-reduce.1
where the time goes:
time: 196 us
  waiting for transfers between devices  121 us (62%)
  blocking collectives  45.9 us (23%)
  between operations  14.1 us (7%)
  matrix products  10.7 us (5%)
  local copies, waits for them, and re-layouts  2.17 us (1%)
    psum x1, waiting for transfers between devices, shards(): sketched = lax.psum(local_sketch, ('blk', 'grp'))  121 us
    all_gather x1, blocking collectives, shards(): lax.all_gather(sources, ('blk', 'grp'), axis=1, tiled=True)  45.9 us
    dot_general x2, matrix products, kernel_terms(): jnp.dot(weights_block, kernel, precision=lax.Precision.HIGHEST, preferred...  4 us
  transfers between devices with their start and end apart: 1, of which 1 were waited for; matrix products, arithmetic and copies ran while one was open for 0% of the time, Pallas kernels for 0%

commit v1 on v0

--- a/solution.py
+++ b/solution.py
@@ -58,7 +58,7 @@
     sources = jnp.concatenate([points, shape_scale[None, :], krylov_basis[KRYLOV - 1]], axis=0)
     empty = jnp.zeros((SYSTEMS, own_count), jnp.float32)
     summed = accumulate(
-        empty, points, labels, lax.all_gather(sources, ("blk", "grp"), axis=1, tiled=True)
+        empty, points, labels, jnp.concatenate(jax.lax.all_gather(sources, ("blk", "grp")), 1)
     )
     image = summed / math.sqrt(everything)
     local_sketch = lax.dot_general(

time: 196 us -> 198 us (1.010)
  no operation moved by 1% of the time
where the time goes in v1:
time: 198 us
  waiting for transfers between devices  121 us (61%)
  blocking collectives  45.9 us (23%)
  between operations  14.1 us (7%)
  matrix products  10.7 us (5%)
  local copies, waits for them, and re-layouts  3.84 us (2%)
    psum x1, waiting for transfers between devices, shards(): sketched = lax.psum(local_sketch, ('blk', 'grp'))  121 us
    all_gather x1, blocking collectives, shards(): jax.lax.all_gather(sources, ('blk', 'grp'))  45.9 us
    dot_general x2, matrix products, kernel_terms(): jnp.dot(weights_block, kernel, precision=lax.Precision.HIGHEST, preferred...  3.99 us
  transfers between devices with their start and end apart: 1, of which 1 were waited for; matrix products, arithmetic and copies ran while one was open for 0% of the time, Pallas kernels for 0%

profile of v1, /device:TPU:0, one launch (start us, length us, event | category | flops | bytes accessed | tf_op | source)
XLA Modules:
  0.0 197.5 jit_solution(17060423394985711732)
XLA Ops:
  7.2 0.0 copy-start
  7.2 0.0 all-reduce.2.cloned.1.call-start
  7.2 0.0 copy-start.4
  7.2 0.8 slice_bitcast_fusion.3
  8.1 0.0 copy-done.4
  8.1 0.7 copy-done.7
  8.7 45.9 %all-gather.1 = f32[32,36,128]{2,1,0:T(8,128)S(1)} all-gather(f32[1,36,128]{2,1,0:T(8,128)S(1)} %maximum_bitcast_fusion), channel_id=2, replica_groups=mesh['blk'=4,'grp'=8] {'blk','grp'}, dimensions={0}, use_global_device_ids=true | all-gather | bytes 608256 | tf_op jit(solution)/shard_map/all_gather | solution.py:61
  54.6 0.1 copy.11
  54.8 0.1 pad.3
  54.8 0.4 copy.19
  55.2 0.0 copy-start.8
  55.2 0.6 copy-done.8
  55.9 4.4 %while.21 = (s32[]{:T(128)}, f32[32,128]{1,0:T(8,128)S(1)}, f32[36,4096]{1,0:T(8,128)S(1)}, s32[128]{0:T(128)S(1)}, f32[3,128]{1,0:T(4,128)S(1)}, /*index=5*/s32...) while((s32[]{:T(128)}, f32[32,128]{1,0:T(8,128)S(1)}, ...), condition=%wide.region_1.0_spmd.clone, body=%wide.region_0.1_spmd.clone.sunk | while | flops 104870024 | bytes 423805 | solution.py:47
  55.9 0.1 constant_dynamic-slice_fusion.2
  56.0 2.0 %convolution_add_fusion.2 = f32[32,128]{1,0:T(8,128)S(1)} fusion(f32[2048]{0:T(1024)S(1)} %bitcast.51, f32[128]{0:T(128)S(1)} %get-tuple-element.195, f32[2048]{0:T(1024)S(1)} %bitcast.54, f32[128]{0:T(128)S(1)} %get-tuple-element.197, f32[2048]{0:T(1024)S(1)} %bitcast.53, f32[128]{0:T(128)S(1)} %get-tuple-element.199, f32[2048]{0:T(1024)S(1)} %bitcast.52, ...), kind=kOutput, calls=%fused_computation.2.clone.1 | convolution fusion | flops 104865792 | bytes 337929 | tf_op jit(solution)/shard_map/while/body/eval_jaxpr/while/body/eval_jaxpr/dot_general | solution.py:25
  58.1 0.1 constant_dynamic-slice_fusion.2
  58.2 2.0 %convolution_add_fusion.2 = f32[32,128]{1,0:T(8,128)S(1)} fusion(f32[2048]{0:T(1024)S(1)} %bitcast.51, f32[128]{0:T(128)S(1)} %get-tuple-element.195, f32[2048]{0:T(1024)S(1)} %bitcast.54, f32[128]{0:T(128)S(1)} %get-tuple-element.197, f32[2048]{0:T(1024)S(1)} %bitcast.53, f32[128]{0:T(128)S(1)} %get-tuple-element.199, f32[2048]{0:T(1024)S(1)} %bitcast.52, ...), kind=kOutput, calls=%fused_computation.2.clone.1 | convolution fusion | flops 104865792 | bytes 337929 | tf_op jit(solution)/shard_map/while/body/eval_jaxpr/while/body/eval_jaxpr/dot_general | solution.py:25
  60.3 0.0 copy-done.2
  60.3 1.3 fusion.32
  61.5 0.0 all-reduce.2.cloned.1.call-update
  61.6 120.9 %all-reduce.2.cloned.1.call-done = f32[32,1024]{1,0:T(8,128)} async-done(((f32[32,1024]{1,0:T(8,128)}), f32[32,1024]{1,0:T(8,128)}) %all-reduce.2.cloned.1.call-update) | async-done | bytes 131088 | tf_op jit(solution)/shard_map/psum | solution.py:71
  182.4 0.0 copy-done
  182.5 3.5 %fusion.27 = f32[32,1,8]{2,1,0:T(1,128)S(1)} fusion(f32[8,32,1024]{2,1,0:T(8,128)S(1)} %copy-done, f32[32,1024,1]{1,0,2:T(8,128)} %bitcast.48), kind=kOutput, calls=%fused_computation.36 | convolution fusion | flops 3145728 | bytes 1180672 | tf_op jit(solution)/shard_map/jrk,rk->jr/dot_general | solution.py:72
  186.0 0.1 copy.14
  186.1 0.1 copy.15
  186.1 0.5 copy-done.5
  186.7 1.5 fusion.25
  188.2 0.4 fusion.29
  188.6 0.5 copy-done.1
  189.1 0.1 multiply_reduce_fusion
  189.2 0.7 subtract_divide_fusion
  189.9 0.7 broadcast_divide_fusion
  (17 shorter events, 0.1 us)
Async XLA Ops:
  7.2 175.3 %copy-start = (f32[8,32,1024]{2,1,0:T(8,128)S(1)}, f32[8,32,1024]{2,1,0:T(8,128)}, u32[]{:S(2)}) copy-start(f32[8,32,1024]{2,1,0:T(8,128)} %param.13) | copy-start | bytes 3145732
  7.2 175.3 %all-reduce.2.cloned.1.call-start = ((), (), s32[]{:S(2)}) async-start(), calls=%async_computation | async-start | bytes 262144 | tf_op jit(solution)/shard_map/psum | solution.py:71
  7.2 0.8 copy-start.4
  8.0 0.7 copy-start.7
  55.2 0.7 copy-start.8
  55.9 4.4 %copy-start.2 = (f32[1024,128]{1,0:T(8,128)S(1)}, f32[1024,128]{1,0:T(8,128)}, u32[]{:S(2)}) copy-start(f32[1024,128]{1,0:T(8,128)} %param.12) | copy-start | bytes 1572868
  186.1 0.6 copy-start.5
  186.7 1.5 copy-start.3
  188.2 0.9 copy-start.1
  189.2 0.7 copy-start.6
Sparse Core Ops, SparseCore 0:
  61.7 120.7 all-reduce.1
